TPU v7x, 32 devices: a whole 2x2x4 slice. The times are simulated.
32 devices in a mesh: dp: 4 (over x, y), ep: 8 (over z, core).
Axes of the slice: x: 2, y: 2, z: 4, core: 2. Of those that a mesh axis runs over, the one named last changes fastest.
Arguments:
- x: bfloat16 [4, 8, 256, 3072], P('dp', 'ep'), parts along dimension 0
- expert: int32 [4, 8, 256, 4], P('dp', 'ep'), parts along dimension 0
- slot: int32 [4, 8, 256, 4], P('dp', 'ep'), parts along dimension 0
- gate: float32 [4, 8, 256, 4], P('dp', 'ep'), parts along dimension 0
- w_gate: bfloat16 [16, 3072, 10752], P('ep')
- w_up: bfloat16 [16, 3072, 10752], P('ep')
- w_down: bfloat16 [16, 10752, 3072], P('ep')
Outputs:
- y: bfloat16 [4, 8, 256, 3072], P('dp', 'ep'), parts along dimension 0
There are 4 independent parts. A program takes and returns all parts, laid end to end along the dimension named above; an argument that names none is the same for every part.
All inputs are finite; a program needn't handle non-finite values.
Results may differ from a plain program's by a relative error of at most 0.009.
Values are sent between devices in bfloat16 or wider.
A program may use at most 2 GiB of HBM per device.

v0:
```python
import functools

import jax
import jax.numpy as jnp
from jax import lax
from jax.experimental import pallas as pl
from jax.experimental.pallas import tpu as pltpu
from jax.sharding import PartitionSpec as P

D, FF, TOK, SLOTS, LOCAL = 3072, 10752, 256, 80, 2
ROWS = 8 * SLOTS
TILE = 512
NT = FF // TILE
DT = 256
TILES = D // DT
SLOT = 6
DEEP = 5

EARLY, EXTRA = 9, 3
PASSES = [(0, EARLY, 480, 640), (EARLY, NT, 320, 640), (0, EXTRA, 160, 480), (EXTRA, EARLY, 0, 480), (0, EXTRA, 0, 160),
          (EARLY, NT, 0, 320)]
ITEMS = 2 * sum(p[1] - p[0] for p in PASSES)
FORWARD, LATER = 16, 34
DEPTH = 3
MESH = pl.DeviceIdType.MESH


def dot(a, b):
    return jnp.dot(a, b, preferred_element_type=jnp.float32)


def tile_of(g):
    tile, start = 0, 0
    for first, last, _, _ in PASSES:
        tile = jnp.where(g >= start, first + (g - start) // 2, tile)
        start += 2 * (last - first)
    return tile


def gate_up_kernel(x_ref, meta_ref, wg_hbm, wu_hbm, h_hbm, c_ref, x_in, meta_in, z_ref, w_ref, h_ref, w_sem, h_sem,
                   x_send, x_recv, meta_send, meta_recv):
    dp, me = lax.axis_index("dp"), lax.axis_index("ep")
    z, core = me // 2, me % 2
    mid = (z == 1) | (z == 2)
    end = jnp.logical_not(mid)
    sibling = me + 1 - 2 * core
    partner = me + 2 - 4 * (z % 2)
    across = jnp.where(z == 1, me + 2, jnp.where(z == 2, me - 2, me))
    chips = (3 - 3 * (z // 2), 2 - z // 2, z + 1 - 2 * (z % 2), z)
    sources = [2 * c + k for c in chips for k in (core, 1 - core)]

    def w_copies(g):
        columns = pl.ds(pl.multiple_of(tile_of(g) * TILE, TILE), TILE)
        at = g % DEPTH
        return [
            pltpu.make_async_copy(hbm.at[g % 2, :, columns], w_ref.at[at, i], w_sem.at[at, i])
            for i, hbm in enumerate((wg_hbm, wu_hbm))
        ]

    def x_copy(i, src, slot, to):
        return pltpu.make_async_remote_copy(
            src_ref=src,
            dst_ref=x_in.at[slot],
            send_sem=x_send.at[i],
            recv_sem=x_recv.at[slot],
            device_id=(dp, to),
            device_id_type=MESH,
        )

    to_sibling = x_copy(0, x_ref, 0, sibling)
    to_partner = x_copy(1, x_ref, 1, partner)
    to_across = x_copy(2, x_ref, 3, across)
    pass_partner = x_copy(3, x_in.at[1], 2, sibling)
    partner_across = x_copy(4, x_in.at[1], 5, across)
    near_out = x_copy(5, x_in.at[3], 3, partner)
    pass_near = x_copy(6, x_in.at[3], 4, sibling)
    far_out = x_copy(7, x_in.at[5], 5, partner)
    pass_far = x_copy(8, x_in.at[5], 6, sibling)

    def meta_copy(k):
        return pltpu.make_async_remote_copy(
            src_ref=meta_ref,
            dst_ref=meta_in.at[me],
            send_sem=meta_send.at[k],
            recv_sem=meta_recv.at[me],
            device_id=(dp, (me + k) % 8),
            device_id_type=MESH,
        )

    def meta_arrival(k):
        source = (me + k) % 8
        return pltpu.make_async_remote_copy(
            src_ref=meta_ref,
            dst_ref=meta_in.at[source],
            send_sem=meta_send.at[k],
            recv_sem=meta_recv.at[source],
            device_id=(dp, source),
            device_id_type=MESH,
        )

    for g in range(DEPTH - 1):
        for copy in w_copies(g):
            copy.start()

    barrier = pltpu.get_barrier_semaphore()
    for k in range(1, 8):
        pl.semaphore_signal(barrier, inc=1, device_id=(dp, (me + k) % 8), device_id_type=MESH)
    pl.semaphore_wait(barrier, 7)

    for k in range(1, 8):
        meta_copy(k).start()
    to_partner.start()

    @pl.when(mid)
    def _():
        to_across.start()

    to_sibling.start()
    meta_in[me] = meta_ref[...]
    for k in range(1, 8):
        meta_arrival(k).wait_recv()

    def match(b, rows):
        meta = meta_in[sources[b]]
        slot = LOCAL * SLOTS * me + lax.broadcasted_iota(jnp.int32, (rows, TOK), 0)
        slot = slot.astype(jnp.float32)
        hits = [slot == jnp.broadcast_to(meta[j : j + 1], (rows, TOK)) for j in range(4)]
        return hits, [jnp.broadcast_to(meta[4 + j : 5 + j], (rows, TOK)) for j in range(4)]

    def dispatch(b, x):
        hits, _ = match(b, LOCAL * SLOTS)
        hit = hits[0] | hits[1] | hits[2] | hits[3]
        rows = dot(jnp.where(hit, 1.0, 0.0).astype(jnp.bfloat16), x[...]).astype(jnp.bfloat16)
        for e in range(LOCAL):
            z_ref[e, b * SLOTS : (b + 1) * SLOTS, :] = rows[e * SLOTS : (e + 1) * SLOTS]

    def forward():
        to_partner.wait_recv()
        pass_partner.start()

        @pl.when(mid)
        def _():
            partner_across.start()
            to_across.wait_recv()
            near_out.start()
            pass_near.start()

    def later():
        @pl.when(mid)
        def _():
            partner_across.wait_recv()
            far_out.start()
            pass_far.start()

        @pl.when(end)
        def _():
            near_out.wait_recv()
            pass_near.start()

    def run(p, start):
        first, last, low, high = PASSES[p]
        rows, count = high - low, 2 * (last - first)

        def h_copy(g):
            columns = pl.ds(pl.multiple_of(tile_of(g) * TILE, TILE), TILE)
            return pltpu.make_async_copy(
                h_ref.at[g % 2, 0:rows], h_hbm.at[g % 2, low:high, columns], h_sem.at[g % 2]
            )

        def item(g, _):
            for copy in w_copies(g):
                copy.wait()

            @pl.when(g + DEPTH - 1 < ITEMS)
            def _():
                for copy in w_copies(g + DEPTH - 1):
                    copy.start()

            if start <= FORWARD < start + count:
                pl.when(g == FORWARD)(forward)
            if start <= LATER < start + count:
                pl.when(g == LATER)(later)

            at = g % DEPTH
            z_rows = z_ref[g % 2, low:high, :]
            gate = dot(z_rows, w_ref[at, 0])
            up = dot(z_rows, w_ref[at, 1])

            @pl.when(g >= start + 2)
            def _():
                h_copy(g - 2).wait()

            h_ref[g % 2, 0:rows, :] = (jax.nn.silu(gate) * up).astype(jnp.bfloat16)
            h_copy(g).start()
            return 0

        lax.fori_loop(start, start + count, item, 0)
        h_copy(start + count - 2).wait()
        h_copy(start + count - 1).wait()
        return start + count

    dispatch(6, x_ref)
    to_sibling.wait_recv()
    dispatch(7, x_in.at[0])
    g = run(0, 0)

    dispatch(4, x_in.at[1])
    pass_partner.wait_recv()
    dispatch(5, x_in.at[2])
    g = run(1, g)

    dispatch(2, x_in.at[3])
    pass_near.wait_recv()
    dispatch(3, x_in.at[4])
    g = run(2, g)

    @pl.when(end)
    def _():
        far_out.wait_recv()
        pass_far.start()

    for b in range(8):
        hits, gates = match(b, 256)
        weight = sum(jnp.where(hit, w, 0.0) for hit, w in zip(hits, gates))
        c_ref[b] = jnp.transpose(weight).astype(jnp.bfloat16)
    dispatch(0, x_in.at[5])
    pass_far.wait_recv()
    dispatch(1, x_in.at[6])
    g = run(3, g)
    g = run(4, g)
    run(5, g)

    for k in range(1, 8):
        meta_copy(k).wait_send()
    for copy in (to_sibling, to_partner, pass_partner, pass_near, pass_far):
        copy.wait_send()

    @pl.when(mid)
    def _():
        for copy in (to_across, partner_across, near_out, far_out):
            copy.wait_send()


def gate_up(x, meta, wg, wu):
    bf16 = jnp.bfloat16
    vmem, hbm = pl.BlockSpec(memory_space=pltpu.VMEM), pl.BlockSpec(memory_space=pl.ANY)
    return pl.pallas_call(
        gate_up_kernel,
        in_specs=[vmem, vmem, hbm, hbm],
        out_specs=[hbm, vmem],
        out_shape=[
            jax.ShapeDtypeStruct((LOCAL, ROWS, FF), bf16),
            jax.ShapeDtypeStruct((8, TOK, TOK), bf16),
        ],
        scratch_shapes=[
            pltpu.VMEM((7, TOK, D), bf16),
            pltpu.VMEM((8, 8, TOK), jnp.float32),
            pltpu.VMEM((LOCAL, ROWS, D), bf16),
            pltpu.VMEM((DEPTH, 2, D, TILE), bf16),
            pltpu.VMEM((2, 480, TILE), bf16),
            pltpu.SemaphoreType.DMA((DEPTH, 2)),
            pltpu.SemaphoreType.DMA((2,)),
            pltpu.SemaphoreType.DMA((9,)),
            pltpu.SemaphoreType.DMA((7,)),
            pltpu.SemaphoreType.DMA((8,)),
            pltpu.SemaphoreType.DMA((8,)),
        ],
        cost_estimate=pl.CostEstimate(
            flops=4 * LOCAL * ROWS * D * FF, bytes_accessed=8 * LOCAL * D * FF, transcendentals=0
        ),
        compiler_params=pltpu.CompilerParams(vmem_limit_bytes=67_000_000, collective_id=2, has_side_effects=True),
        name="gate_up",
    )(x, meta, wg, wu)


def down_kernel(c_ref, h_hbm, w_hbm, y_ref, h_ref, w_ref, out_ref, s_ref, swap_out, fn_out, tu_out, v_out,
                swap_in, fn_in, tu_in, v_in, h_sem, w_sem, send_sem, recv_sem):
    dp, me = lax.axis_index("dp"), lax.axis_index("ep")
    z = me // 2
    mid = (z == 1) | (z == 2)
    sibling = me + 1 - 2 * (me % 2)
    partner = me + 2 - 4 * (z % 2)
    across = jnp.where(z == 1, me + 2, jnp.where(z == 2, me - 2, me))

    def h_copy(e):
        return pltpu.make_async_copy(h_hbm.at[e], h_ref.at[e], h_sem.at[e])

    def w_copy(n, e):
        columns = pl.ds(pl.multiple_of(n * DT, DT), DT)
        return pltpu.make_async_copy(w_hbm.at[e, :, columns], w_ref.at[e], w_sem.at[e])

    def send(kind, n, src, dst, to):
        return pltpu.make_async_remote_copy(
            src_ref=src.at[n % 2],
            dst_ref=dst.at[n % SLOT],
            send_sem=send_sem.at[kind, n % 2],
            recv_sem=recv_sem.at[kind, n % SLOT],
            device_id=(dp, to),
            device_id_type=pl.DeviceIdType.MESH,
        )

    swap_copy = lambda n: send(0, n, swap_out, swap_in, sibling)
    fn_copy = lambda n: send(1, n, fn_out, fn_in, partner)
    tu_copy = lambda n: send(2, n, tu_out, tu_in, across)
    v_copy = lambda n: send(3, n, v_out, v_in, partner)

    h_copy(0).start()
    w_copy(0, 0).start()
    h_copy(1).start()
    w_copy(0, 1).start()

    barrier = pltpu.get_barrier_semaphore()
    for to in (sibling, partner):
        pl.semaphore_signal(barrier, inc=1, device_id=(dp, to), device_id_type=pl.DeviceIdType.MESH)

    @pl.when(mid)
    def _():
        pl.semaphore_signal(barrier, inc=1, device_id=(dp, across), device_id_type=pl.DeviceIdType.MESH)
        pl.semaphore_wait(barrier, 3)

    @pl.when(jnp.logical_not(mid))
    def _():
        pl.semaphore_wait(barrier, 2)

    h_copy(0).wait()

    def project(n, e):
        w_copy(n, e).wait()
        out = dot(h_ref[e], w_ref[e]).astype(jnp.bfloat16)
        for b in range(8):
            out_ref[b, e * SLOTS : (e + 1) * SLOTS, :] = out[b * SLOTS : (b + 1) * SLOTS]

        @pl.when(n + 1 < TILES)
        def _():
            w_copy(n + 1, e).start()

    def step(n, _):
        @pl.when(n < TILES)
        def _():
            project(n, 0)

        @pl.when((n >= 1) & (n < TILES + 1))
        def _():
            k = n - 1
            swap_copy(k).wait_recv()
            at, got = k % DEEP, k % SLOT
            for q in range(4):
                s_ref[at, q] += swap_in[got, q].astype(jnp.float32)

            @pl.when(jnp.logical_not(mid))
            def _():
                @pl.when(k >= 2)
                def _():
                    fn_copy(k - 2).wait_send()

                fn_out[k % 2] = s_ref[at, 0:2].astype(jnp.bfloat16)
                fn_copy(k).start()

        @pl.when((n >= 2) & (n < TILES + 2) & mid)
        def _():
            k = n - 2
            at, got = k % DEEP, k % SLOT
            fn_copy(k).wait_recv()

            @pl.when(k >= 2)
            def _():
                tu_copy(k - 2).wait_send()

            tu_out[k % 2] = (s_ref[at, 0:2] + fn_in[got].astype(jnp.float32)).astype(jnp.bfloat16)
            tu_copy(k).start()

        @pl.when((n >= 3) & (n < TILES + 3))
        def _():
            k = n - 3
            at, got = k % DEEP, k % SLOT

            @pl.when(mid)
            def _():
                tu_copy(k).wait_recv()
                s_ref[at, 2] += tu_in[got, 0].astype(jnp.float32)
                s_ref[at, 3] += tu_in[got, 1].astype(jnp.float32)

            @pl.when(k >= 2)
            def _():
                v_copy(k - 2).wait_send()

            v_out[k % 2] = s_ref[at, 2].astype(jnp.bfloat16)
            v_copy(k).start()

        @pl.when(n >= 4)
        def _():
            k = n - 4
            at, got = k % DEEP, k % SLOT
            v_copy(k).wait_recv()
            columns = pl.ds(pl.multiple_of(k * DT, DT), DT)
            y_ref[:, columns] = (s_ref[at, 3] + v_in[got].astype(jnp.float32)).astype(jnp.bfloat16)

        @pl.when(n < TILES)
        def _():
            @pl.when(n == 0)
            def _():
                h_copy(1).wait()

            project(n, 1)

            @pl.when(n >= 2)
            def _():
                swap_copy(n - 2).wait_send()

            for b in range(8):
                y = dot(c_ref[b, :, 0 : LOCAL * SLOTS], out_ref[b])
                if b % 2:
                    swap_out[n % 2, b // 2] = y.astype(jnp.bfloat16)
                else:
                    s_ref[n % DEEP, b // 2] = y
            swap_copy(n).start()

        return 0

    lax.fori_loop(0, TILES + 4, step, 0)

    for k in (TILES - 2, TILES - 1):
        swap_copy(k).wait_send()
        v_copy(k).wait_send()

        @pl.when(mid)
        def _():
            tu_copy(k).wait_send()

        @pl.when(jnp.logical_not(mid))
        def _():
            fn_copy(k).wait_send()


def down(h, from_slot, wd):
    bf16, part = jnp.bfloat16, (TOK, DT)
    return pl.pallas_call(
        down_kernel,
        in_specs=[
            pl.BlockSpec(memory_space=pltpu.VMEM),
            pl.BlockSpec(memory_space=pl.ANY),
            pl.BlockSpec(memory_space=pl.ANY),
        ],
        out_specs=pl.BlockSpec(memory_space=pltpu.VMEM),
        out_shape=jax.ShapeDtypeStruct((TOK, D), bf16),
        scratch_shapes=[
            pltpu.VMEM((LOCAL, ROWS, FF), bf16),
            pltpu.VMEM((LOCAL, FF, DT), bf16),
            pltpu.VMEM((8, LOCAL * SLOTS, DT), bf16),
            pltpu.VMEM((DEEP, 4, *part), jnp.float32),
            pltpu.VMEM((2, 4, *part), bf16),
            pltpu.VMEM((2, 2, *part), bf16),
            pltpu.VMEM((2, 2, *part), bf16),
            pltpu.VMEM((2, *part), bf16),
            pltpu.VMEM((SLOT, 4, *part), bf16),
            pltpu.VMEM((SLOT, 2, *part), bf16),
            pltpu.VMEM((SLOT, 2, *part), bf16),
            pltpu.VMEM((SLOT, *part), bf16),
            pltpu.SemaphoreType.DMA((LOCAL,)),
            pltpu.SemaphoreType.DMA((LOCAL,)),
            pltpu.SemaphoreType.DMA((4, 2)),
            pltpu.SemaphoreType.DMA((4, SLOT)),
        ],
        cost_estimate=pl.CostEstimate(
            flops=2 * LOCAL * ROWS * FF * D, bytes_accessed=2 * LOCAL * FF * D, transcendentals=0
        ),
        compiler_params=pltpu.CompilerParams(
            vmem_limit_bytes=67_000_000, collective_id=1, has_side_effects=True
        ),
        name="down",
    )(from_slot, h, wd)


def layer(x, expert, slot, gate, wg, wu, wd):
    x, expert, slot, gate = x[0, 0], expert[0, 0], slot[0, 0], gate[0, 0]
    key = jnp.where(slot < SLOTS, expert * SLOTS + slot, -1).astype(jnp.float32)
    rounded = gate.astype(jnp.bfloat16).astype(jnp.float32)
    meta = jnp.concatenate([key.T, rounded.T], 0)
    h, from_slot = gate_up(x, meta, wg, wu)
    return down(h, from_slot, wd)[None, None]


def solution(mesh):
    spec = P("dp", "ep")
    return jax.shard_map(
        layer,
        mesh=mesh,
        in_specs=(spec, spec, spec, spec, P("ep"), P("ep"), P("ep")),
        out_specs=spec,
        check_vma=False,
    )
```

profile of v0, /device:TPU:0, one launch (start us, length us, event | category | flops | bytes accessed | tf_op | source)
XLA Modules:
  0.0 379.5 jit_solution(6024524039505116856)
XLA Ops:
  0.0 0.7 convert_bitcast_fusion.1
  0.7 0.7 convert_bitcast_fusion
  1.4 0.6 pad_maximum_fusion.meta_ref
  2.0 237.6 %gate_up.1 = (bf16[2,640,10752]{2,1,0:T(8,128)(2,1)}, bf16[8,256,256]{2,1,0:T(8,128)(2,1)}) custom-call(bf16[256,3072]{1,0:T(8,128)(2,1)} %bitcast.12, f32[8,256]{1,0:T(8,128)} %pad_maximum_fusion.meta_ref, bf16[2,3072,10752]{2,1,0:T(8,128)(2,1)} %wg_hbm.1, bf16[2,3072,10752]{2,1,0:T(8,128)(2,1)} %wu_hbm.1), custom_call_target="tpu_custom_call" | custom-call | flops 169114337280 | bytes 528482304 | tf_op jit(solution)/shard_map/gate_up/pallas_call | solution.py:247
  239.7 137.1 %down.1 = bf16[256,3072]{1,0:T(8,128)(2,1)} custom-call(bf16[8,256,256]{2,1,0:T(8,128)(2,1)} %get-tuple-element.7.c_ref, bf16[2,640,10752]{2,1,0:T(8,128)(2,1)} %get-tuple-element.8.h_hbm, bf16[2,10752,3072]{2,1,0:T(8,128)(2,1)} %w_hbm.1), custom_call_target="tpu_custom_call" | custom-call | flops 84557168640 | bytes 132120576 | tf_op jit(solution)/shard_map/down/pallas_call | solution.py:437
  376.8 2.7 copy.9
where the time goes:
time: 380 us; the launch traced here: 379 us
  Pallas kernels  375 us (99%)
    pallas_call x1, Pallas kernels, gate_up(): pl.pallas_call(gate_up_kernel, in_specs=[vmem, vmem, hbm, hbm], out_specs...  238 us
    pallas_call x1, Pallas kernels, down(): pl.pallas_call(down_kernel, in_specs=[pl.BlockSpec(memory_space=pltpu.VME...  137 us

commit v1 on v0

--- a/solution.py
+++ b/solution.py
@@ -1,5 +1,3 @@
-import functools
-
 import jax
 import jax.numpy as jnp
 from jax import lax
@@ -20,8 +18,8 @@
 PASSES = [(0, EARLY, 480, 640), (EARLY, NT, 320, 640), (0, EXTRA, 160, 480), (EXTRA, EARLY, 0, 480), (0, EXTRA, 0, 160),
           (EARLY, NT, 0, 320)]
 ITEMS = 2 * sum(p[1] - p[0] for p in PASSES)
-FORWARD, LATER = 16, 34
-DEPTH = 3
+FORWARD, LATER = 16, 32
+DEPTH = 5
 MESH = pl.DeviceIdType.MESH
 
 
@@ -291,23 +289,28 @@
 
     def send(kind, n, src, dst, to):
         return pltpu.make_async_remote_copy(
-            src_ref=src.at[n % 2],
-            dst_ref=dst.at[n % SLOT],
+            src_ref=src,
+            dst_ref=dst,
             send_sem=send_sem.at[kind, n % 2],
             recv_sem=recv_sem.at[kind, n % SLOT],
             device_id=(dp, to),
             device_id_type=pl.DeviceIdType.MESH,
         )
 
-    swap_copy = lambda n: send(0, n, swap_out, swap_in, sibling)
-    fn_copy = lambda n: send(1, n, fn_out, fn_in, partner)
-    tu_copy = lambda n: send(2, n, tu_out, tu_in, across)
-    v_copy = lambda n: send(3, n, v_out, v_in, partner)
+    def swap_copy(n):
+        return send(0, n, swap_out.at[n % 2], swap_in.at[n % SLOT], sibling)
+
+    def fn_copy(n, i):
+        return send(1 + i, n, fn_out.at[n % 2, i], fn_in.at[n % SLOT, i], partner)
+
+    def tu_copy(n, i):
+        return send(3 + i, n, tu_out.at[n % 2, i], tu_in.at[n % SLOT, i], across)
+
+    def v_copy(n):
+        return send(5, n, v_out.at[n % 2], v_in.at[n % SLOT], partner)
 
     h_copy(0).start()
     w_copy(0, 0).start()
-    h_copy(1).start()
-    w_copy(0, 1).start()
 
     barrier = pltpu.get_barrier_semaphore()
     for to in (sibling, partner):
@@ -323,6 +326,8 @@
         pl.semaphore_wait(barrier, 2)
 
     h_copy(0).wait()
+    h_copy(1).start()
+    w_copy(0, 1).start()
 
     def project(n, e):
         w_copy(n, e).wait()
@@ -349,25 +354,28 @@
 
             @pl.when(jnp.logical_not(mid))
             def _():
+                for i in range(2):
+
+                    @pl.when(k >= 2)
+                    def _():
+                        fn_copy(k - 2, i).wait_send()
+
+                    fn_out[k % 2, i] = s_ref[at, i].astype(jnp.bfloat16)
+                    fn_copy(k, i).start()
+
+        @pl.when((n >= 2) & (n < TILES + 2) & mid)
+        def _():
+            k = n - 2
+            at, got = k % DEEP, k % SLOT
+            for i in range(2):
+                fn_copy(k, i).wait_recv()
+
                 @pl.when(k >= 2)
                 def _():
-                    fn_copy(k - 2).wait_send()
-
-                fn_out[k % 2] = s_ref[at, 0:2].astype(jnp.bfloat16)
-                fn_copy(k).start()
-
-        @pl.when((n >= 2) & (n < TILES + 2) & mid)
-        def _():
-            k = n - 2
-            at, got = k % DEEP, k % SLOT
-            fn_copy(k).wait_recv()
-
-            @pl.when(k >= 2)
-            def _():
-                tu_copy(k - 2).wait_send()
-
-            tu_out[k % 2] = (s_ref[at, 0:2] + fn_in[got].astype(jnp.float32)).astype(jnp.bfloat16)
-            tu_copy(k).start()
+                    tu_copy(k - 2, i).wait_send()
+
+                tu_out[k % 2, i] = (s_ref[at, i] + fn_in[got, i].astype(jnp.float32)).astype(jnp.bfloat16)
+                tu_copy(k, i).start()
 
         @pl.when((n >= 3) & (n < TILES + 3))
         def _():
@@ -376,9 +384,8 @@
 
             @pl.when(mid)
             def _():
-                tu_copy(k).wait_recv()
+                tu_copy(k, 0).wait_recv()
                 s_ref[at, 2] += tu_in[got, 0].astype(jnp.float32)
-                s_ref[at, 3] += tu_in[got, 1].astype(jnp.float32)
 
             @pl.when(k >= 2)
             def _():
@@ -386,6 +393,11 @@
 
             v_out[k % 2] = s_ref[at, 2].astype(jnp.bfloat16)
             v_copy(k).start()
+
+            @pl.when(mid)
+            def _():
+                tu_copy(k, 1).wait_recv()
+                s_ref[at, 3] += tu_in[got, 1].astype(jnp.float32)
 
         @pl.when(n >= 4)
         def _():
@@ -425,11 +437,13 @@
 
         @pl.when(mid)
         def _():
-            tu_copy(k).wait_send()
+            tu_copy(k, 0).wait_send()
+            tu_copy(k, 1).wait_send()
 
         @pl.when(jnp.logical_not(mid))
         def _():
-            fn_copy(k).wait_send()
+            fn_copy(k, 0).wait_send()
+            fn_copy(k, 1).wait_send()
 
 
 def down(h, from_slot, wd):
@@ -458,8 +472,8 @@
             pltpu.VMEM((SLOT, *part), bf16),
             pltpu.SemaphoreType.DMA((LOCAL,)),
             pltpu.SemaphoreType.DMA((LOCAL,)),
-            pltpu.SemaphoreType.DMA((4, 2)),
-            pltpu.SemaphoreType.DMA((4, SLOT)),
+            pltpu.SemaphoreType.DMA((6, 2)),
+            pltpu.SemaphoreType.DMA((6, SLOT)),
         ],
         cost_estimate=pl.CostEstimate(
             flops=2 * LOCAL * ROWS * FF * D, bytes_accessed=2 * LOCAL * FF * D, transcendentals=0

time: 380 us -> 374 us (0.984)
  Pallas kernels: 375 us -> 369 us
    pallas_call x1, Pallas kernels: 137 us -> 133 us  [down(): pl.pallas_call(down_kernel, in_specs=[pl.BlockSpec(memory_space=pltpu.VME...]
where the time goes in v1:
time: 374 us; the launch traced here: 373 us
  Pallas kernels  369 us (99%)
    pallas_call x1, Pallas kernels, gate_up(): pl.pallas_call(gate_up_kernel, in_specs=[vmem, vmem, hbm, hbm], out_specs...  235 us
    pallas_call x1, Pallas kernels, down(): pl.pallas_call(down_kernel, in_specs=[pl.BlockSpec(memory_space=pltpu.VME...  133 us

profile of v1, /device:TPU:0, one launch (start us, length us, event | category | flops | bytes accessed | tf_op | source)
XLA Modules:
  0.0 373.5 jit_solution(12076799071445873383)
XLA Ops:
  0.0 0.7 convert_bitcast_fusion.1
  0.7 0.7 convert_bitcast_fusion
  1.4 0.6 pad_maximum_fusion.meta_ref
  2.0 235.5 %gate_up.1 = (bf16[2,640,10752]{2,1,0:T(8,128)(2,1)}, bf16[8,256,256]{2,1,0:T(8,128)(2,1)}) custom-call(bf16[256,3072]{1,0:T(8,128)(2,1)} %bitcast.12, f32[8,256]{1,0:T(8,128)} %pad_maximum_fusion.meta_ref, bf16[2,3072,10752]{2,1,0:T(8,128)(2,1)} %wg_hbm.1, bf16[2,3072,10752]{2,1,0:T(8,128)(2,1)} %wu_hbm.1), custom_call_target="tpu_custom_call" | custom-call | flops 169114337280 | bytes 528482304 | tf_op jit(solution)/shard_map/gate_up/pallas_call | solution.py:245
  237.5 133.3 %down.1 = bf16[256,3072]{1,0:T(8,128)(2,1)} custom-call(bf16[8,256,256]{2,1,0:T(8,128)(2,1)} %get-tuple-element.7.c_ref, bf16[2,640,10752]{2,1,0:T(8,128)(2,1)} %get-tuple-element.8.h_hbm, bf16[2,10752,3072]{2,1,0:T(8,128)(2,1)} %w_hbm.1), custom_call_target="tpu_custom_call" | custom-call | flops 84557168640 | bytes 132120576 | tf_op jit(solution)/shard_map/down/pallas_call | solution.py:451
  370.8 2.7 copy.9
